TPU v7x, 32 devices: a whole 2x2x4 slice. The times are simulated.
32 devices in a mesh: ep: 32 (over z, y, x, core).
Axes of the slice: x: 2, y: 2, z: 4, core: 2. Of those that a mesh axis runs over, the one named last changes fastest.
Arguments:
- x_tokens: bfloat16 [32768, 1536], P('ep')
- w_router: bfloat16 [1536, 64], replicated
- w_gate: bfloat16 [64, 1536, 512], P('ep')
- w_up: bfloat16 [64, 1536, 512], P('ep')
- w_down: bfloat16 [64, 512, 1536], P('ep')
- topk_idx: int32 [32768, 6], P('ep')
- dy_tokens: bfloat16 [32768, 1536], P('ep')
Outputs:
- output 1: bfloat16 [32768, 1536], P('ep')
- output 2: float32 [], replicated
- output 3: bfloat16 [32768, 1536], P('ep')
- output 4: float32 [1536, 64], replicated
- output 5: float32 [64, 1536, 512], P('ep')
- output 6: float32 [64, 1536, 512], P('ep')
- output 7: float32 [64, 512, 1536], P('ep')
All inputs are finite; a program needn't handle non-finite values.
Results may differ from a plain program's by a relative error of at most 0.00525984.
Values are sent between devices in bfloat16 or wider.
A program may use at most 1 GiB of HBM per device.

v0:
```python
import jax
import jax.numpy as jnp
from jax import lax
from jax.sharding import PartitionSpec as P

AUX_COEF = 0.001


def route_slots(idx_dev, n_exp, capacity):
    tok_count, top_k = idx_dev.shape
    choice_mask = idx_dev[:, :, None] == jnp.arange(n_exp, dtype=jnp.int32)
    expert_hot = jnp.sum(choice_mask.astype(jnp.int32), axis=1)
    earlier = jnp.cumsum(expert_hot, axis=0) - expert_hot
    position = jnp.take_along_axis(earlier, idx_dev, axis=1)
    slot_ids = jnp.where(position < capacity, idx_dev * capacity + position, n_exp * capacity)
    pair_ids = jnp.arange(tok_count * top_k, dtype=jnp.int32)
    empty_fill = jnp.full((n_exp * capacity,), tok_count * top_k, jnp.int32)
    pair_of_slot = empty_fill.at[slot_ids.reshape(-1)].set(pair_ids, mode="drop")
    return slot_ids, pair_of_slot, choice_mask, expert_hot


def solution(mesh):
    n_dev = mesh.shape["ep"]

    def local_block(x_loc, w_router, wg_loc, wu_loc, wd_loc, idx_loc, dy_loc):
        tok_count, model_dim = x_loc.shape
        top_k = idx_loc.shape[1]
        n_exp = w_router.shape[1]
        loc_exp = wg_loc.shape[0]
        capacity = (5 * tok_count * top_k + 4 * n_exp - 1) // (4 * n_exp)
        n_total = tok_count * n_dev
        logits = jnp.dot(x_loc, w_router, preferred_element_type=jnp.float32)
        router_prob = jax.nn.softmax(logits, axis=-1)
        pick_prob = jnp.take_along_axis(router_prob, idx_loc, axis=1)
        pick_sum = jnp.sum(pick_prob, axis=1, keepdims=True)
        gate_f32 = pick_prob / pick_sum
        gate_bf = gate_f32.astype(jnp.bfloat16)
        slot_ids, pair_of_slot, choice_mask, expert_hot = route_slots(idx_loc, n_exp, capacity)
        tok_of_slot = pair_of_slot // top_k
        buf_shape = (n_dev, loc_exp, capacity, model_dim)

        send_x = jnp.take(x_loc, tok_of_slot, axis=0, mode="fill", fill_value=0).reshape(buf_shape)
        recv_x = lax.all_to_all(send_x, "ep", 0, 1)
        gate_pre = jnp.einsum("egcd,edf->egcf", recv_x, wg_loc, preferred_element_type=jnp.float32)
        up_pre = jnp.einsum("egcd,edf->egcf", recv_x, wu_loc, preferred_element_type=jnp.float32)
        act_gate = jax.nn.silu(gate_pre)
        hidden = (act_gate * up_pre).astype(jnp.bfloat16)
        out_slot = jnp.einsum("egcf,efd->egcd", hidden, wd_loc, preferred_element_type=jnp.float32).astype(jnp.bfloat16)
        back_out = lax.all_to_all(out_slot, "ep", 1, 0).reshape(n_exp * capacity, model_dim)
        out_tok = jnp.take(back_out, slot_ids, axis=0, mode="fill", fill_value=0)
        y_loc = jnp.einsum("tk,tkd->td", gate_bf, out_tok, preferred_element_type=jnp.float32).astype(jnp.bfloat16)

        load_stats = jnp.concatenate([jnp.sum(expert_hot, axis=0).astype(jnp.float32), jnp.sum(router_prob, axis=0)])
        load_stats = lax.psum(load_stats, "ep")
        load_frac = load_stats[:n_exp] / (n_total * top_k)
        mean_prob = load_stats[n_exp:] / n_total
        aux_loss = AUX_COEF * n_exp * jnp.sum(load_frac * mean_prob)

        gate_slot = jnp.take(gate_bf.reshape(-1), pair_of_slot, mode="fill", fill_value=0)
        dy_slot = jnp.take(dy_loc, tok_of_slot, axis=0, mode="fill", fill_value=0)
        send_do = (gate_slot[:, None] * dy_slot).reshape(buf_shape)
        recv_do = lax.all_to_all(send_do, "ep", 0, 1)
        dw_down = jnp.einsum("egcf,egcd->efd", hidden, recv_do, preferred_element_type=jnp.float32)
        d_hidden = jnp.einsum("egcd,efd->egcf", recv_do, wd_loc, preferred_element_type=jnp.float32).astype(jnp.bfloat16).astype(jnp.float32)
        sigmoid_g = jax.nn.sigmoid(gate_pre)
        d_gate_pre = (d_hidden * up_pre * sigmoid_g * (1.0 + gate_pre * (1.0 - sigmoid_g))).astype(jnp.bfloat16)
        d_up_pre = (d_hidden * act_gate).astype(jnp.bfloat16)
        dw_gate = jnp.einsum("egcd,egcf->edf", recv_x, d_gate_pre, preferred_element_type=jnp.float32)
        dw_up = jnp.einsum("egcd,egcf->edf", recv_x, d_up_pre, preferred_element_type=jnp.float32)
        dx_slot = (jnp.einsum("egcf,edf->egcd", d_gate_pre, wg_loc, preferred_element_type=jnp.float32)
                   + jnp.einsum("egcf,edf->egcd", d_up_pre, wu_loc, preferred_element_type=jnp.float32)).astype(jnp.bfloat16)
        back_dx = lax.all_to_all(dx_slot, "ep", 1, 0).reshape(n_exp * capacity, model_dim)
        dx_tok = jnp.take(back_dx, slot_ids, axis=0, mode="fill", fill_value=0)
        dx_expert = jnp.sum(dx_tok, axis=1, dtype=jnp.float32)

        d_gate = jnp.einsum("tkd,td->tk", out_tok, dy_loc, preferred_element_type=jnp.float32)
        d_pick = (d_gate - jnp.sum(d_gate * gate_f32, axis=1, keepdims=True)) / pick_sum
        d_prob = jnp.sum(jnp.where(choice_mask, d_pick[:, :, None], 0.0), axis=1) + AUX_COEF * n_exp * load_frac / n_total
        d_logit = router_prob * (d_prob - jnp.sum(router_prob * d_prob, axis=1, keepdims=True))
        d_logit_bf = d_logit.astype(jnp.bfloat16)
        dw_router = lax.psum(jnp.einsum("td,te->de", x_loc, d_logit_bf, preferred_element_type=jnp.float32), "ep")
        dx_loc = (dx_expert + jnp.einsum("te,de->td", d_logit_bf, w_router, preferred_element_type=jnp.float32)).astype(jnp.bfloat16)
        return y_loc, aux_loss, dx_loc, dw_router, dw_gate, dw_up, dw_down

    tok_spec = P("ep")
    return jax.shard_map(
        local_block,
        mesh=mesh,
        in_specs=(tok_spec, P(), tok_spec, tok_spec, tok_spec, tok_spec, tok_spec),
        out_specs=(tok_spec, P(), tok_spec, P(), tok_spec, tok_spec, tok_spec),
        check_vma=False,
    )
```

profile of v0, /device:TPU:0, one launch (start us, length us, event | category | flops | bytes accessed | tf_op | source)
XLA Modules:
  0.0 2859.3 jit_solution(2613862658910844618)
XLA Ops:
  8.1 1.6 convert_reduce_fusion.1
  11.2 31.1 %reduce-window.6 = s32[64,8,128]{2,1,0:T(8,128)S(1)} reduce-window(s32[64,8,128]{2,1,0:T(8,128)} %bitcast.136, s32[]{:T(128)} %constant.60.clone.1), window={size=1x1x128 pad=0_0x0_0x127_0}, to_apply=%region_4.5 | reduce-window | flops 8323072 | bytes 524292 | tf_op jit(solution)/shard_map/reduce-window
  46.5 1.4 reshape.148
  47.9 49.3 %gather_fusion.2 = s32[6144]{0:T(1024)S(1)} fusion(s32[1024,64]{0,1:T(8,128)S(1)} %fusion.49, s32[6144]{0:T(1024)S(1)} %reshape.148), kind=kCustom, calls=%fused_computation.6 | custom fusion | bytes 98304 | tf_op jit(solution)/shard_map/jit(take_along_axis)/gather | solution.py:14
  97.2 1.3 reshape.157
  98.5 1.2 copy.68
  101.4 1.4 reshape.107
  102.9 23.0 scatter_custom_fusion
  127.2 3.0 fusion.65
  130.9 49.3 %gather_fusion.1 = f32[6144]{0:T(1024)S(1)} fusion(f32[1024,64]{0,1:T(8,128)S(1)} %get-tuple-element.12, s32[6144]{0:T(1024)S(1)} %reshape.148), kind=kCustom, calls=%fused_computation.5 | custom fusion | bytes 98304 | tf_op jit(solution)/shard_map/jit(take_along_axis)/gather | solution.py:34
  180.2 1.3 reshape.151
  181.5 1.2 copy.65
  184.8 45.1 %gather_fusion = bf16[7680]{0:T(1024)(128)(2,1)S(1)} fusion(bf16[6144]{0:T(1024)(128)(2,1)S(1)} %convert_element_type.52, s32[8192]{0:T(1024)S(1)} %pad_clamp_fusion), kind=kCustom, calls=%fused_computation.4 | custom fusion | bytes 61440 | tf_op jit(solution)/shard_map/jit(_take)/gather | solution.py:59
  229.9 48.6 %gather_fusion.3 = bf16[7680,1536]{1,0:T(8,128)(2,1)} fusion(bf16[1024,1536]{1,0:T(8,128)(2,1)} %param.11, s32[8192]{0:T(1024)S(1)} %pad_clamp_fusion.1), kind=kCustom, calls=%fused_computation.clone | custom fusion | bytes 47216640 | tf_op jit(solution)/shard_map/jit(_take)/gather | solution.py:42
  278.5 48.6 %gather_fusion.5 = bf16[7680,1536]{1,0:T(8,128)(2,1)} fusion(bf16[1024,1536]{1,0:T(8,128)(2,1)} %param.17, s32[8192]{0:T(1024)S(1)} %pad_clamp_fusion.1), kind=kCustom, calls=%fused_computation.2.clone | custom fusion | bytes 47216640 | tf_op jit(solution)/shard_map/jit(_take)/gather | solution.py:60
  327.1 32.5 %select_multiply_fusion = (bf16[7680,1536]{1,0:T(8,128)(2,1)}, bf16[7680,1536]{1,0:T(8,128)(2,1)}) fusion(bf16[7680,1536]{1,0:T(8,128)(2,1)} %gather_fusion.5, pred[7680]{0:T(1024)(128)(4,1)S(1)} %copy-done.22, bf16[7680]{0:T(1024)(128)(2,1)S(1)} %and_select_fusion, bf16[7680,1536]{1,0:T(8,128)(2,1)} %gather_fusion.3), kind=kLoop, calls=%fused_computation.24 | loop fusion | flops 35389440 | bytes 94394880 | tf_op jit(solution)/shard_map/mul | solution.py:61
  359.6 527.9 %all_to_all.60 = bf16[32,2,1,120,1536]{4,3,1,2,0:T(8,128)(2,1)} all-to-all(bf16[32,2,1,120,1536]{4,3,1,2,0:T(8,128)(2,1)} %bitcast.132), channel_id=1, replica_groups=mesh['ep'=32] {'ep'}, dimensions={0} | all-to-all | bytes 47185920 | tf_op jit(solution)/shard_map/all_to_all | solution.py:62
  887.6 4.2 all-to-all-start
  891.8 19.9 fusion.30
  911.7 468.2 %all-to-all-done = bf16[32,2,1,120,1536]{4,3,1,2,0:T(8,128)(2,1)} async-done(((bf16[32,2,1,120,1536]{4,3,1,2,0:T(8,128)(2,1)}), bf16[32,2,1,120,1536]{4,3,1,2,0:T(8,128)(2,1)}, u32[]{:S(2)}, u32[]{:S(2)}) %all-to-all-start) | async-done | bytes 23592992 | tf_op jit(solution)/shard_map/all_to_all | solution.py:43
  1380.0 21.2 fusion.10
  1401.1 28.6 %fusion.20 = (bf16[2,32,120,512]{3,2,1,0:T(8,128)(2,1)}, bf16[2,32,120,512]{3,2,1,0:T(8,128)(2,1)}) fusion(bf16[2,32,120,512]{3,2,1,0:T(8,128)(2,1)} %fusion.30, f32[2,32,120,512]{3,2,1,0:T(8,128)} %fusion.10, bf16[2,1536,512]{2,1,0:T(8,128)(2,1)S(1)} %copy-done, bf16[32,2,1,120,1536]{4,3,1,2,0:T(8,128)(2,1)} %all-to-all-done), kind=kOutput, calls=%fused_computation.36 | convolution fusion | flops 12134645760 | bytes 66060288 | tf_op jit(solution)/shard_map/egcd,edf->egcf/dot_general | solution.py:45
  1429.7 20.2 fusion.15
  1449.9 19.9 copy.73
  1469.8 32.2 %all-to-all-start.1 = ((bf16[1,2,32,120,1536]{4,3,1,0,2:T(8,128)(2,1)}), bf16[1,2,32,120,1536]{4,3,1,0,2:T(8,128)(2,1)}, u32[]{:S(2)}, u32[]{:S(2)}) async-start(bf16[1,2,32,120,1536]{4,3,1,0,2:T(8,128)(2,1)} %copy.73), calls=%async_computation.1 | async-start | bytes 47185920 | tf_op jit(solution)/shard_map/all_to_all | solution.py:49
  1502.0 23.5 fusion.44
  1525.6 36.9 %fusion.14 = bf16[1,2,32,120,1536]{4,3,2,1,0:T(8,128)(2,1)} fusion(f32[2,32,120,1536]{3,2,1,0:T(8,128)} %fusion.44, bf16[2,1536,512]{2,1,0:T(8,128)(2,1)S(1)} %copy-done, bf16[2,32,120,512]{3,2,1,0:T(8,128)(2,1)} %fusion.30, f32[2,32,120,512]{3,2,1,0:T(8,128)} %fusion.10), kind=kOutput, calls=%fused_computation.28 | convolution fusion | flops 12130713600 | bytes 97517568 | tf_op jit(solution)/shard_map/egcf,edf->egcd/dot_general | solution.py:71
  1562.5 19.9 copy.79
  1582.4 406.3 %all-to-all-done.1 = bf16[1,2,32,120,1536]{4,3,1,0,2:T(8,128)(2,1)} async-done(((bf16[1,2,32,120,1536]{4,3,1,0,2:T(8,128)(2,1)}), bf16[1,2,32,120,1536]{4,3,1,0,2:T(8,128)(2,1)}, u32[]{:S(2)}, u32[]{:S(2)}) %all-to-all-start.1) | async-done | bytes 23592992 | tf_op jit(solution)/shard_map/all_to_all | solution.py:49
  1988.7 29.5 %all-to-all-start.3 = ((bf16[1,2,32,120,1536]{4,3,1,0,2:T(8,128)(2,1)}), bf16[1,2,32,120,1536]{4,3,1,0,2:T(8,128)(2,1)}, u32[]{:S(2)}, u32[]{:S(2)}) async-start(bf16[1,2,32,120,1536]{4,3,1,0,2:T(8,128)(2,1)} %copy.79), calls=%async_computation.3 | async-start | bytes 47185920 | tf_op jit(solution)/shard_map/all_to_all | solution.py:72
  2020.2 1.4 reshape.182
  2021.6 1.1 copy.84
  2022.9 531.1 %psum.14 = f32[128]{0:T(128)S(1)} all-reduce(f32[128]{0:T(128)S(1)} %pad_maximum_fusion), channel_id=1, replica_groups=mesh['ep'=32] {'ep'}, use_global_device_ids=true, to_apply=%region_9.12 | all-reduce | flops 128 | bytes 1024 | tf_op jit(solution)/shard_map/psum | solution.py:54
  2555.7 19.6 fusion.39
  2575.3 19.6 fusion.33
  2595.0 22.8 fusion.36
  2617.7 48.0 %gather_fusion.4 = bf16[6144,1536]{1,0:T(8,128)(2,1)} fusion(bf16[7680,1536]{1,0:T(8,128)(2,1)} %bitcast.22, s32[6144]{0:T(1024)S(1)} %broadcast_clamp_fusion), kind=kCustom, calls=%fused_computation.1.clone | custom fusion | bytes 37773312 | tf_op jit(solution)/shard_map/jit(_take)/gather | solution.py:50
  2665.8 29.2 %reshape.185 = bf16[1024,6,1536]{2,1,0:T(8,128)(2,1)} reshape(bf16[6144,1536]{1,0:T(8,128)(2,1)} %gather_fusion.4) | data formatting | bytes 37748736 | tf_op jit(solution)/shard_map/jit(_take)/gather | solution.py:50
  2695.0 19.9 fusion.12
  2714.9 1.4 copy.87
  2717.5 3.3 convolution_bitcast_fusion
  2720.8 14.0 fusion.13
  2734.9 48.1 %gather_fusion.6 = bf16[6144,1536]{1,0:T(8,128)(2,1)} fusion(bf16[7680,1536]{1,0:T(8,128)(2,1)} %bitcast.35, s32[6144]{0:T(1024)S(1)} %broadcast_clamp_fusion), kind=kCustom, calls=%fused_computation.3.clone | custom fusion | bytes 37773312 | tf_op jit(solution)/shard_map/jit(_take)/gather | solution.py:73
  2783.0 29.2 %reshape.191 = bf16[1024,6,1536]{2,1,0:T(8,128)(2,1)} reshape(bf16[6144,1536]{1,0:T(8,128)(2,1)} %gather_fusion.6) | data formatting | bytes 37748736 | tf_op jit(solution)/shard_map/jit(_take)/gather | solution.py:73
  2812.2 26.2 convert_reduce_fusion
  2838.4 5.4 add_convert_fusion.1
  2843.8 5.3 copy.131
  2849.1 1.8 copy.133
  (95 shorter events, 16.7 us)
Async XLA Ops:
  7.2 1394.0 %copy-start = (bf16[2,1536,512]{2,1,0:T(8,128)(2,1)S(1)}, bf16[2,1536,512]{2,1,0:T(8,128)(2,1)}, u32[]{:S(2)}) copy-start(bf16[2,1536,512]{2,1,0:T(8,128)(2,1)} %param.14) | copy-start | bytes 9437188
  9.7 0.7 copy-start.3
  47.9 51.8 %copy-start.7 = (s32[1024,6]{0,1:T(8,128)S(1)}, s32[1024,6]{0,1:T(8,128)}, u32[]{:S(2)}) copy-start(s32[1024,6]{0,1:T(8,128)} %param.16) | copy-start | bytes 73732
  100.3 2.5 copy-start.13
  125.9 4.3 copy-start.11
  130.9 49.3 %copy-start.1 = (f32[1024,64]{0,1:T(8,128)}, f32[1024,64]{0,1:T(8,128)S(1)}, u32[]{:S(2)}) copy-start(f32[1024,64]{0,1:T(8,128)S(1)} %get-tuple-element.12) | copy-start | bytes 786436
  130.9 51.8 %copy-start.17 = (pred[1024,6]{0,1:T(8,128)(4,1)S(1)}, pred[1024,6]{0,1:T(8,128)(4,1)}, u32[]{:S(2)}) copy-start(pred[1024,6]{0,1:T(8,128)(4,1)} %get-tuple-element.15) | copy-start | bytes 18436
  180.2 49.7 %copy-start.12 = (s32[7680]{0:T(1024)S(1)}, s32[7680]{0:T(1024)}, u32[]{:S(2)}) copy-start(s32[7680]{0:T(1024)} %copy-done.11) | copy-start | bytes 92164
  180.2 49.7 %copy-start.19 = (s32[7680]{0:T(1024)S(1)}, s32[7680]{0:T(1024)}, u32[]{:S(2)}) copy-start(s32[7680]{0:T(1024)} %get-tuple-element.17) | copy-start | bytes 92164
  182.7 0.6 copy-start.9
  183.4 1.4 copy-start.20
  183.4 95.1 %copy-start.15 = (bf16[1024,6]{0,1:T(8,128)(2,1)}, bf16[1024,6]{0,1:T(8,128)(2,1)S(1)}, u32[]{:S(2)}) copy-start(bf16[1024,6]{0,1:T(8,128)(2,1)S(1)} %fusion.58) | copy-start | bytes 36868
  278.5 48.6 %copy-start.22 = (pred[7680]{0:T(1024)(128)(4,1)S(1)}, pred[7680]{0:T(1024)(128)(4,1)}, u32[]{:S(2)}) copy-start(pred[7680]{0:T(1024)(128)(4,1)} %get-tuple-element.16) | copy-start | bytes 23044
  887.6 492.4 %all-to-all-start = ((bf16[32,2,1,120,1536]{4,3,1,2,0:T(8,128)(2,1)}), bf16[32,2,1,120,1536]{4,3,1,2,0:T(8,128)(2,1)}, u32[]{:S(2)}, u32[]{:S(2)}) async-start(bf16[32,2,1,120,1536]{4,3,1,2,0:T(8,128)(2,1)} %bitcast.131), calls=%async_computation | async-start | bytes 47185920 | tf_op jit(solution)/shard_map/all_to_all | solution.py:43
  1469.8 519.0 %all-to-all-start.1 = ((bf16[1,2,32,120,1536]{4,3,1,0,2:T(8,128)(2,1)}), bf16[1,2,32,120,1536]{4,3,1,0,2:T(8,128)(2,1)}, u32[]{:S(2)}, u32[]{:S(2)}) async-start(bf16[1,2,32,120,1536]{4,3,1,0,2:T(8,128)(2,1)} %copy.73), calls=%async_computation.1 | async-start | bytes 47185920 | tf_op jit(solution)/shard_map/all_to_all | solution.py:49
  1582.4 435.9 %copy-start.25 = (s32[64]{0:T(128)S(1)}, s32[64]{0:T(128)}, u32[]{:S(2)}) copy-start(s32[64]{0:T(128)} %get-tuple-element.9) | copy-start | bytes 772
  1582.4 435.9 %copy-start.23 = (pred[1024,6]{0,1:T(8,128)(4,1)S(1)}, pred[1024,6]{0,1:T(8,128)(4,1)}, u32[]{:S(2)}) copy-start(pred[1024,6]{0,1:T(8,128)(4,1)} %get-tuple-element.13) | copy-start | bytes 18436
  1582.4 436.8 %copy-start.14 = (s32[1024,6]{0,1:T(8,128)S(1)}, s32[1024,6]{0,1:T(8,128)}, u32[]{:S(2)}) copy-start(s32[1024,6]{0,1:T(8,128)} %copy-done.13) | copy-start | bytes 73732
  1582.4 439.2 %copy-start.16 = (bf16[1024,6]{0,1:T(8,128)(2,1)S(1)}, bf16[1024,6]{0,1:T(8,128)(2,1)}, u32[]{:S(2)}) copy-start(bf16[1024,6]{0,1:T(8,128)(2,1)} %copy-done.15) | copy-start | bytes 36868
  1582.4 440.4 %copy-start.26 = (f32[64]{0:T(128)S(1)}, f32[64]{0:T(128)}, u32[]{:S(2)}) copy-start(f32[64]{0:T(128)} %get-tuple-element.11) | copy-start | bytes 772
  1988.7 746.1 %all-to-all-start.3 = ((bf16[1,2,32,120,1536]{4,3,1,0,2:T(8,128)(2,1)}), bf16[1,2,32,120,1536]{4,3,1,0,2:T(8,128)(2,1)}, u32[]{:S(2)}, u32[]{:S(2)}) async-start(bf16[1,2,32,120,1536]{4,3,1,0,2:T(8,128)(2,1)} %copy.79), calls=%async_computation.3 | async-start | bytes 47185920 | tf_op jit(solution)/shard_map/all_to_all | solution.py:72
  2018.2 830.9 %all-reduce.2.cloned.1.call-start = ((), (), s32[]{:S(2)}) async-start(), calls=%async_computation.4 | async-start | bytes 786432 | tf_op jit(solution)/shard_map/psum | solution.py:81
  2695.0 21.4 copy-start.10
  2695.0 21.4 copy-start.18
  2695.0 21.4 copy-start.21
  2695.0 21.4 copy-start.8
  2695.0 21.6 copy-start.2
  2695.0 21.6 copy-start.24
  2716.9 0.7 copy-start.4
  2812.2 26.2 copy-start.5
  2812.2 26.2 copy-start.6
Sparse Core Ops, SparseCore 0:
  2721.0 127.5 all-reduce.1
where the time goes:
time: 2870 us; the launch traced here: 2860 us
  blocking collectives  1060 us (37%)
  waiting for transfers between devices  875 us (30%)
  local copies, waits for them, and re-layouts  486 us (17%)
  matrix products  258 us (9%)
  other arithmetic  98.7 us (3%)
  starting transfers between devices  66 us (2%)
    psum x1, blocking collectives, local_block(): load_stats = lax.psum(load_stats, 'ep')  531 us
    all_to_all x1, blocking collectives, local_block(): recv_do = lax.all_to_all(send_do, 'ep', 0, 1)  528 us
    all_to_all x1, waiting for transfers between devices, local_block(): recv_x = lax.all_to_all(send_x, 'ep', 0, 1)  468 us
    all_to_all x1, waiting for transfers between devices, local_block(): lax.all_to_all(out_slot, 'ep', 1, 0).reshape(n_exp * capacity, model_dim)  406 us
    gather x2, local copies, waits for them, and re-layouts, local_block(): dx_tok = jnp.take(back_dx, slot_ids, axis=0, mode='fill', fill_value=0)  77.3 us
    gather x2, local copies, waits for them, and re-layouts, local_block(): out_tok = jnp.take(back_out, slot_ids, axis=0, mode='fill', fill_value=0)  77.2 us
  transfers between devices with their start and end apart: 4, of which 2 were waited for; matrix products, arithmetic and copies ran while one was open for 14% of the time, Pallas kernels for 0%

commit v1 on v0

v1 whole, which is shorter than its diff:
```python
import functools

import jax
import jax.numpy as jnp
from jax import lax
from jax.experimental import pallas as pl
from jax.experimental.pallas import tpu as pltpu
from jax.sharding import PartitionSpec as P

AUX_COEF = 0.001
N_PLANE = 8
X_PIECES = 2
Y_PIECES = 2
DX_PIECES = 4
F32 = jnp.float32
BF16 = jnp.bfloat16


def one_hot_rows(pos, capacity):
    n, _, tok = pos.shape
    slot = lax.broadcasted_iota(jnp.int32, (n, capacity, tok), 1).astype(F32)
    return slot == pos


def dispatch_kernel(capacity, weighted, pos_ref, wt_ref, x_ref, out0_ref, out1_ref):
    n_dst = pos_ref.shape[2]
    tok = x_ref.shape[1]
    for g, out_ref in enumerate((out0_ref, out1_ref)):
        mask = one_hot_rows(pos_ref[0, g], capacity)
        value = jnp.broadcast_to(wt_ref[0, g], mask.shape) if weighted else jnp.ones(mask.shape, F32)
        sel = jnp.where(mask, value, 0.0).reshape(n_dst * capacity, tok).astype(BF16)
        rows = jnp.dot(sel, x_ref[0], preferred_element_type=F32)
        out_ref[:, 0] = rows.reshape(n_dst, capacity, rows.shape[1]).astype(BF16)


def dispatch(pos, wt, x_line, capacity, weighted):
    n_src, _, n_dst, _, tok = pos.shape
    dim = x_line.shape[2]
    out = jax.ShapeDtypeStruct((n_dst, n_src, capacity, dim), BF16)
    table = pl.BlockSpec((1, 2, n_dst, 1, tok), lambda j: (j, 0, 0, 0, 0))
    out_spec = pl.BlockSpec((n_dst, 1, capacity, dim), lambda j: (0, j, 0, 0))
    return pl.pallas_call(
        functools.partial(dispatch_kernel, capacity, weighted),
        grid=(n_src,),
        in_specs=[table, table, pl.BlockSpec((1, tok, dim), lambda j: (j, 0, 0))],
        out_specs=[out_spec, out_spec],
        out_shape=[out, out],
        compiler_params=pltpu.CompilerParams(vmem_limit_bytes=60 * 2**20),
        cost_estimate=pl.CostEstimate(flops=4 * n_src * n_dst * capacity * tok * dim, bytes_accessed=36 * 2**20, transcendentals=0),
    )(pos, wt, x_line)


def combine_kernel(capacity, weighted, with_dot, pos_ref, wt_ref, rows0_ref, rows1_ref, *refs):
    dy_ref, acc_ref, a_ref = refs if with_dot else (None, refs[0], None)
    n, _, tok = pos_ref.shape[2:]
    for g, rows_ref in enumerate((rows0_ref, rows1_ref)):
        mask = one_hot_rows(pos_ref[0, g], capacity)
        value = jnp.broadcast_to(wt_ref[0, g], mask.shape) if weighted else jnp.ones(mask.shape, F32)
        sel = jnp.where(mask, value, 0.0).reshape(n * capacity, tok).astype(BF16)
        rows = rows_ref[:, 0].astype(F32).reshape(n * capacity, rows_ref.shape[3]).astype(BF16)
        part = lax.dot_general(sel, rows, (((0,), (0,)), ((), ())), preferred_element_type=F32)
        if g == 0:
            acc_ref[0] = part
        else:
            acc_ref[0] += part
        if with_dot:
            prod = lax.dot_general(rows, dy_ref[0], (((1,), (1,)), ((), ())), preferred_element_type=F32)
            prod = jnp.where(mask, prod.reshape(n, capacity, tok), 0.0)
            a_ref[0, g] = jnp.sum(prod, axis=1)


def combine(pos, wt, rows0, rows1, dy_line, piece, capacity, weighted):
    n_src, _, n_dst, _, tok = pos.shape
    dim = rows0.shape[3]
    table = pl.BlockSpec((1, 2, n_dst, 1, tok), lambda j: (j, 0, 0, 0, 0))
    rows_spec = pl.BlockSpec((n_dst, 1, capacity, dim), lambda j: (0, j, 0, 0))
    by_src = pl.BlockSpec((1, tok, dim), lambda j: (j, 0, 0))
    in_specs = [table, table, rows_spec, rows_spec]
    operands = [pos, wt, rows0, rows1]
    out_shape = [jax.ShapeDtypeStruct((n_src, tok, dim), F32)]
    out_specs = [by_src]
    with_dot = dy_line is not None
    if with_dot:
        in_specs.append(pl.BlockSpec((1, tok, dim), lambda j: (j, 0, piece)))
        operands.append(dy_line)
        out_shape.append(jax.ShapeDtypeStruct((n_src, 2, n_dst, tok), F32))
        out_specs.append(pl.BlockSpec((1, 2, n_dst, tok), lambda j: (j, 0, 0, 0)))
    flops = 4 * n_src * n_dst * capacity * tok * dim * (2 if with_dot else 1)
    return pl.pallas_call(
        functools.partial(combine_kernel, capacity, weighted, with_dot),
        grid=(n_src,),
        in_specs=in_specs,
        out_specs=out_specs,
        out_shape=out_shape,
        compiler_params=pltpu.CompilerParams(vmem_limit_bytes=63 * 2**20),
        cost_estimate=pl.CostEstimate(flops=flops, bytes_accessed=50 * 2**20, transcendentals=0),
    )(*operands)


def solution(mesh):
    n_dev = mesh.shape["ep"]
    n_line = n_dev // N_PLANE
    lines = [[z * N_PLANE + i for z in range(n_line)] for i in range(N_PLANE)]
    planes = [[z * N_PLANE + i for i in range(N_PLANE)] for z in range(n_line)]

    def local_block(x_loc, w_router, wg_loc, wu_loc, wd_loc, idx_loc, dy_loc):
        tok, dim = x_loc.shape
        top_k = idx_loc.shape[1]
        n_exp = w_router.shape[1]
        loc_exp = wg_loc.shape[0]
        capacity = (5 * tok * top_k + 4 * n_exp - 1) // (4 * n_exp)
        n_total = tok * n_dev
        me = lax.axis_index("ep")

        def columns(pieces):
            return [slice(i * dim // pieces, (i + 1) * dim // pieces) for i in range(pieces)]

        def after(value, earlier_value):
            return lax.optimization_barrier((value, earlier_value))[0]

        x_line = []
        for cols in columns(X_PIECES):
            part = x_loc[:, cols] if not x_line else after(x_loc[:, cols], x_line[-1])
            x_line.append(lax.all_gather(part, "ep", axis_index_groups=lines))
        dy_line = lax.all_gather(after(dy_loc, x_line[-1]), "ep", axis_index_groups=lines)

        logits = lax.dot_general(w_router, x_loc, (((0,), (1,)), ((), ())), preferred_element_type=F32)
        prob = jax.nn.softmax(logits, axis=0)
        idx_t = idx_loc.T
        hot = jnp.any(idx_t[:, None, :] == jnp.arange(n_exp, dtype=jnp.int32)[None, :, None], axis=0)
        hot_f = hot.astype(F32)
        before = (jnp.arange(tok)[:, None] < jnp.arange(tok)[None, :]).astype(BF16)
        earlier = jnp.dot(hot.astype(BF16), before, preferred_element_type=F32)
        pick_sum = jnp.sum(jnp.where(hot, prob, 0.0), axis=0, keepdims=True)
        gate = jnp.where(hot, prob, 0.0) / pick_sum
        gate_bf = gate.astype(BF16)
        kept = hot & (earlier < capacity)
        pos = jnp.where(kept, earlier, -1.0)

        count = jnp.sum(hot_f, axis=1)
        load = lax.psum(jnp.concatenate([count, jnp.sum(prob, axis=1)]), "ep")
        load_frac = load[:n_exp] / (n_total * top_k)
        mean_prob = load[n_exp:] / n_total
        aux_loss = AUX_COEF * n_exp * jnp.sum(load_frac * mean_prob)

        tables = jnp.stack([pos.astype(BF16), gate_bf]).reshape(2, n_line, N_PLANE, loc_exp, tok)
        tables = lax.all_to_all(after(tables.transpose(1, 0, 3, 2, 4), load), "ep", 0, 0, axis_index_groups=lines)
        tables = tables.astype(F32)[:, :, :, :, None, :]
        pos_line, gate_line = tables[:, 0], tables[:, 1]

        done = []

        def in_plane(rows, then=()):
            rows = rows.reshape(N_PLANE, n_line, capacity, rows.shape[-1])
            rows = after(rows, (done[-1:], then))
            rows = lax.all_to_all(rows, "ep", 0, 0, axis_index_groups=planes)
            done.append(rows)
            return rows

        def in_plane_rows(rows):
            return in_plane(rows).reshape(n_dev * capacity, rows.shape[-1])

        def sum_line(parts):
            return lax.psum_scatter(parts, "ep", axis_index_groups=lines)

        parts = []
        for x_part in x_line:
            send_x = dispatch(pos_line, gate_line, x_part, capacity, False)
            parts.append([in_plane_rows(rows) for rows in send_x])
        recv_x = [jnp.concatenate([p[g] for p in parts], axis=1) for g in range(loc_exp)]
        pre_gate, pre_up, hidden = [], [], []
        for g in range(loc_exp):
            pg = jnp.dot(recv_x[g], wg_loc[g], preferred_element_type=F32)
            pu = jnp.dot(recv_x[g], wu_loc[g], preferred_element_type=F32)
            pre_gate.append(pg)
            pre_up.append(pu)
            hidden.append((jax.nn.silu(pg) * pu).astype(BF16))

        y_sums, dots = [], 0.0
        send_o = [[jnp.dot(hidden[g], wd_loc[g, :, cols], preferred_element_type=F32).astype(BF16) for g in range(loc_exp)]
                  for cols in columns(Y_PIECES)]
        for i in range(Y_PIECES):
            back = []
            for g in range(loc_exp):
                then = send_o[i + 1][0] if g + 1 == loc_exp and i + 1 < Y_PIECES else ()
                back.append(in_plane(send_o[i][g], then))
            y_part, dot_part = combine(pos_line, gate_line, back[0], back[1], dy_line, i, capacity, True)
            y_sums.append(sum_line(y_part))
            dots += dot_part
        y_loc = jnp.concatenate(y_sums, axis=1).astype(BF16)

        send_d = dispatch(pos_line, gate_line, dy_line, capacity, True)
        recv_d = [in_plane_rows(rows) for rows in send_d]
        d_gate_rows, d_up_rows, dwg, dwu, dwd = [], [], [], [], []
        for g in range(loc_exp):
            dg_rows = recv_d[g]
            d_hidden = lax.dot_general(dg_rows, wd_loc[g], (((1,), (1,)), ((), ())), preferred_element_type=F32).astype(BF16).astype(F32)
            sig = jax.nn.sigmoid(pre_gate[g])
            d_pg = (d_hidden * pre_up[g] * sig * (1.0 + pre_gate[g] * (1.0 - sig))).astype(BF16)
            d_pu = (d_hidden * jax.nn.silu(pre_gate[g])).astype(BF16)
            d_gate_rows.append(d_pg)
            d_up_rows.append(d_pu)
            outer = (((0,), (0,)), ((), ()))
            dwd.append(lax.dot_general(hidden[g], dg_rows, outer, preferred_element_type=F32))
            dwg.append(lax.dot_general(recv_x[g], d_pg, outer, preferred_element_type=F32))
            dwu.append(lax.dot_general(recv_x[g], d_pu, outer, preferred_element_type=F32))

        def dx_rows(g, cols):
            rows = (lax.dot_general(d_gate_rows[g], wg_loc[g, cols], (((1,), (1,)), ((), ())), preferred_element_type=F32)
                    + lax.dot_general(d_up_rows[g], wu_loc[g, cols], (((1,), (1,)), ((), ())), preferred_element_type=F32))
            return rows.astype(BF16)

        dx_sums = []
        send_dx = [[dx_rows(g, cols) for g in range(loc_exp)] for cols in columns(DX_PIECES)]
        for i in range(DX_PIECES):
            back = []
            for g in range(loc_exp):
                then = send_dx[i + 1][0] if g + 1 == loc_exp and i + 1 < DX_PIECES else ()
                back.append(in_plane(send_dx[i][g], then))
            dx_part = combine(pos_line, gate_line, back[0], back[1], None, i, capacity, False)[0]
            dx_sums.append(sum_line(dx_part))

        a_pick = lax.all_to_all(after(dots, done[-1]), "ep", 0, 0, axis_index_groups=lines)
        a_pick = a_pick.transpose(0, 2, 1, 3).reshape(n_exp, tok)

        d_pick = (a_pick - jnp.sum(a_pick * gate, axis=0, keepdims=True)) / pick_sum
        d_prob = jnp.where(hot, d_pick, 0.0) + (AUX_COEF * n_exp * load_frac / n_total)[:, None]
        d_logit = (prob * (d_prob - jnp.sum(prob * d_prob, axis=0, keepdims=True))).astype(BF16)
        dx_router = lax.dot_general(d_logit, w_router, (((0,), (1,)), ((), ())), preferred_element_type=F32)
        dx_loc = (jnp.concatenate(dx_sums, axis=1) + dx_router).astype(BF16)

        dwr_part = lax.dot_general(x_loc, d_logit, (((0,), (1,)), ((), ())), preferred_element_type=F32)
        dwr_part = dwr_part.reshape(n_dev, dim // n_dev, n_exp)
        dwr_sum = jnp.sum(lax.all_to_all(dwr_part, "ep", 0, 0), axis=0)
        dw_router = lax.all_gather(dwr_sum, "ep", tiled=True)
        return y_loc, aux_loss, dx_loc, dw_router, jnp.stack(dwg), jnp.stack(dwu), jnp.stack(dwd)

    tok_spec = P("ep")
    return jax.shard_map(
        local_block,
        mesh=mesh,
        in_specs=(tok_spec, P(), tok_spec, tok_spec, tok_spec, tok_spec, tok_spec),
        out_specs=(tok_spec, P(), tok_spec, P(), tok_spec, tok_spec, tok_spec),
        check_vma=False,
    )
```

time: 2870 us -> 1610 us (0.56)
  blocking collectives: 1060 us -> 302 us
  local copies, waits for them, and re-layouts: 486 us -> 17.9 us
  Pallas kernels: 0 us -> 169 us
  waiting for transfers between devices: 875 us -> 738 us
  other arithmetic: 98.7 us -> 28 us
    psum x1, blocking collectives: 531 us -> 48.8 us  [local_block(): load = lax.psum(jnp.concatenate([count, jnp.sum(prob, axis=1)]), 'ep')]
    gather x15 -> x0, local copies, waits for them, and re-layouts: 403 us -> none  [the longest x2 77.3 us: local_block(): dx_tok = jnp.take(back_dx, slot_ids, axis=0, mode='fill', fill_value=0)]
    all_to_all x1 -> x5, blocking collectives: 528 us -> 208 us  [the longest x4 189 us: in_plane(): rows = lax.all_to_all(rows, 'ep', 0, 0, axis_index_groups=planes)]
    all_to_all x3 -> x16, waiting for transfers between devices: 875 us -> 644 us  [the longest x14 624 us: in_plane(): rows = lax.all_to_all(rows, 'ep', 0, 0, axis_index_groups=planes)]
    pallas_call x0 -> x9, Pallas kernels: none -> 169 us  [the longest x6 107 us: combine(): pl.pallas_call(functools.partial(combine_kernel, capacity, weighted, with...]
    all_gather x0 -> x3, waiting for transfers between devices: none -> 76.8 us  [the longest x2 74.5 us: local_block(): x_line.append(lax.all_gather(part, 'ep', axis_index_groups=lines))]
    all_gather x0 -> x1, blocking collectives: none -> 44.8 us  [local_block(): dw_router = lax.all_gather(dwr_sum, 'ep', tiled=True)]
    broadcast_in_dim x3 -> x1, local copies, waits for them, and re-layouts: 41.2 us -> 0.43 us  [local_block(): tables = tables.astype(F32)[:, :, :, :, None, :]]
  transfers between devices with their start and end apart: 4 -> 25, of which waited for: 2 -> 20; matrix products, arithmetic and copies ran while one was open for 14% -> 18% of each run, Pallas kernels for 0% -> 9%
where the time goes in v1:
time: 1610 us; the launch traced here: 1590 us
  waiting for transfers between devices  738 us (46%)
  blocking collectives  302 us (19%)
  matrix products  247 us (15%)
  Pallas kernels  169 us (10%)
  starting transfers between devices  75.9 us (5%)
  other arithmetic  28 us (2%)
  local copies, waits for them, and re-layouts  17.9 us (1%)
  between operations  16.5 us (1%)
    all_to_all x14, waiting for transfers between devices, in_plane(): rows = lax.all_to_all(rows, 'ep', 0, 0, axis_index_groups=planes)  624 us
    all_to_all x4, blocking collectives, in_plane(): rows = lax.all_to_all(rows, 'ep', 0, 0, axis_index_groups=planes)  189 us
    pallas_call x6, Pallas kernels, combine(): pl.pallas_call(functools.partial(combine_kernel, capacity, weighted, with...  107 us
    all_gather x2, waiting for transfers between devices, local_block(): x_line.append(lax.all_gather(part, 'ep', axis_index_groups=lines))  74.5 us
    all_to_all x14, starting transfers between devices, in_plane(): rows = lax.all_to_all(rows, 'ep', 0, 0, axis_index_groups=planes)  67.6 us
    pallas_call x3, Pallas kernels, dispatch(): pl.pallas_call(functools.partial(dispatch_kernel, capacity, weighted), gr...  61.8 us
    psum x1, blocking collectives, local_block(): load = lax.psum(jnp.concatenate([count, jnp.sum(prob, axis=1)]), 'ep')  48.8 us
    all_gather x1, blocking collectives, local_block(): dw_router = lax.all_gather(dwr_sum, 'ep', tiled=True)  44.8 us
  transfers between devices with their start and end apart: 25, of which 20 were waited for; matrix products, arithmetic and copies ran while one was open for 18% of the time, Pallas kernels for 9%

profile of v1, /device:TPU:0, one launch (start us, length us, event | category | flops | bytes accessed | tf_op | source)
XLA Modules:
  0.0 1594.9 jit_solution(9155311723597678297)
XLA Ops:
  14.2 48.8 %psum.7 = f32[128]{0:T(128)} all-reduce(f32[128]{0:T(128)S(1)} %pad_maximum_fusion.6), channel_id=1, replica_groups=mesh['ep'=32] {'ep'}, use_global_device_ids=true, to_apply=%region_6.7 | all-reduce | flops 128 | bytes 1024 | tf_op jit(solution)/shard_map/psum | solution.py:141
  63.1 19.4 %all_to_all.105 = bf16[4,2,2,8,1024]{4,3,2,1,0:T(8,128)(2,1)S(1)} all-to-all(bf16[4,2,2,8,1024]{4,3,2,1,0:T(8,128)(2,1)S(1)} %maximum_bitcast_fusion), channel_id=1, replica_groups={{0,8,16,24},{1,9,17,25},{2,10,18,26},{3,11,19,27},{4,12,20,28},{5,13,21..., dimensions={0} | all-to-all | bytes 524288 | tf_op jit(solution)/shard_map/all_to_all | solution.py:147
  83.7 52.3 %all-gather.7.cloned.1.call-done = bf16[4096,768]{1,0:T(8,128)(2,1)} async-done(((bf16[1024,768]{1,0:T(8,128)(2,1)}), bf16[4096,768]{1,0:T(8,128)(2,1)}) %all-gather.7.cloned.1.call-update) | async-done | bytes 6291472 | tf_op jit(solution)/shard_map/all_gather | solution.py:124
  136.1 16.1 %shard_map.126 = (bf16[8,4,120,768]{3,2,1,0:T(8,128)(2,1)}, bf16[8,4,120,768]{3,2,1,0:T(8,128)(2,1)}) custom-call(f32[4,2,8,1,1024]{4,3,2,1,0:T(1,128)} %get-tuple-element.93.pos_ref, f32[4,2,8,1,1024]{4,3,2,1,0:T(1,128)} %get-tuple-element.92.wt_ref, bf16[4,1024,768]{2,1,0:T(8,128)(2,1)} %bitcast.195), custom_call_target="tpu_custom_call" | custom-call | flops 12079595520 | bytes 37748736 | tf_op jit(solution)/shard_map/pallas_call | solution.py:42
  152.2 72.1 %all_to_all.106 = bf16[8,4,120,768]{3,2,1,0:T(8,128)(2,1)} all-to-all(bf16[8,4,120,768]{3,2,1,0:T(8,128)(2,1)} %get-tuple-element.39), channel_id=1, replica_groups={{0,1,2,3,4,5,6,7},{8,9,10,11,12,13,14,15},{16,17,18,19,20,21,22,23},{24..., dimensions={0} | all-to-all | bytes 11796480 | tf_op jit(solution)/shard_map/all_to_all | solution.py:156
  229.0 22.2 %all-gather.9.cloned.1.call-done = bf16[4096,768]{1,0:T(8,128)(2,1)} async-done(((bf16[1024,768]{1,0:T(8,128)(2,1)}), bf16[4096,768]{1,0:T(8,128)(2,1)}) %all-gather.9.cloned.1.call-update) | async-done | bytes 6291472 | tf_op jit(solution)/shard_map/all_gather | solution.py:124
  251.2 16.0 %shard_map.127 = (bf16[8,4,120,768]{3,2,1,0:T(8,128)(2,1)}, bf16[8,4,120,768]{3,2,1,0:T(8,128)(2,1)}) custom-call(f32[4,2,8,1,1024]{4,3,2,1,0:T(1,128)} %get-tuple-element.93.pos_ref, f32[4,2,8,1,1024]{4,3,2,1,0:T(1,128)} %get-tuple-element.92.wt_ref, bf16[4,1024,768]{2,1,0:T(8,128)(2,1)} %bitcast.196), custom_call_target="tpu_custom_call" | custom-call | flops 12079595520 | bytes 37748736 | tf_op jit(solution)/shard_map/pallas_call | solution.py:42
  267.3 29.0 %all-to-all-done.2 = bf16[8,4,120,768]{3,2,1,0:T(8,128)(2,1)} async-done(((bf16[8,4,120,768]{3,2,1,0:T(8,128)(2,1)}), bf16[8,4,120,768]{3,2,1,0:T(8,128)(2,1)}, u32[]{:S(2)}, u32[]{:S(2)}) %all-to-all-start.2) | async-done | bytes 5898272 | tf_op jit(solution)/shard_map/all_to_all | solution.py:156
  301.7 66.5 %all-to-all-done.3 = bf16[8,4,120,768]{3,2,1,0:T(8,128)(2,1)} async-done(((bf16[8,4,120,768]{3,2,1,0:T(8,128)(2,1)}), bf16[8,4,120,768]{3,2,1,0:T(8,128)(2,1)}, u32[]{:S(2)}, u32[]{:S(2)}) %all-to-all-start.3) | async-done | bytes 5898272 | tf_op jit(solution)/shard_map/all_to_all | solution.py:156
  373.6 12.4 fusion.28
  386.1 13.6 multiply_convert_fusion.1
  399.7 8.3 convolution_convert_fusion.1
  414.1 26.8 %all-to-all-done.4 = bf16[8,4,120,768]{3,2,1,0:T(8,128)(2,1)} async-done(((bf16[8,4,120,768]{3,2,1,0:T(8,128)(2,1)}), bf16[8,4,120,768]{3,2,1,0:T(8,128)(2,1)}, u32[]{:S(2)}, u32[]{:S(2)}) %all-to-all-start.4) | async-done | bytes 5898272 | tf_op jit(solution)/shard_map/all_to_all | solution.py:156
  446.1 11.4 fusion.24
  457.5 13.2 multiply_convert_fusion
  478.9 34.5 %all-to-all-done.5.rows0_ref = bf16[8,4,120,768]{3,2,1,0:T(8,128)(2,1)} async-done(((bf16[8,4,120,768]{3,2,1,0:T(8,128)(2,1)}), bf16[8,4,120,768]{3,2,1,0:T(8,128)(2,1)}, u32[]{:S(2)}, u32[]{:S(2)}) %all-to-all-start.5) | async-done | bytes 5898272 | tf_op jit(solution)/shard_map/all_to_all | solution.py:156
  520.7 64.7 %all-to-all-done.6.rows1_ref = bf16[8,4,120,768]{3,2,1,0:T(8,128)(2,1)} async-done(((bf16[8,4,120,768]{3,2,1,0:T(8,128)(2,1)}), bf16[8,4,120,768]{3,2,1,0:T(8,128)(2,1)}, u32[]{:S(2)}, u32[]{:S(2)}) %all-to-all-start.6) | async-done | bytes 5898272 | tf_op jit(solution)/shard_map/all_to_all | solution.py:156
  585.4 29.3 %shard_map.128 = (f32[4,1024,768]{2,1,0:T(8,128)}, f32[4,2,8,1024]{3,2,1,0:T(8,128)}) custom-call(f32[4,2,8,1,1024]{4,3,2,1,0:T(1,128)} %get-tuple-element.93.pos_ref, f32[4,2,8,1,1024]{4,3,2,1,0:T(1,128)} %get-tuple-element.92.wt_ref, bf16[8,4,120,768]{3,2,1,0:T(8,128)(2,1)} %all-to-all-done.5.rows0_ref, bf16[8,4,120,768]{3,2,1,0:T(8,128)(2,1)} %all-to-all-done.6.rows1_ref, ...), custom_call_target="tpu_custom_call" | custom-call | flops 24159191040 | bytes 52428800 | tf_op jit(solution)/shard_map/pallas_call | solution.py:89
  619.5 8.1 convolution_convert_fusion
  627.6 59.1 %all-to-all-done.7.rows0_ref = bf16[8,4,120,768]{3,2,1,0:T(8,128)(2,1)} async-done(((bf16[8,4,120,768]{3,2,1,0:T(8,128)(2,1)}), bf16[8,4,120,768]{3,2,1,0:T(8,128)(2,1)}, u32[]{:S(2)}, u32[]{:S(2)}) %all-to-all-start.7) | async-done | bytes 5898272 | tf_op jit(solution)/shard_map/all_to_all | solution.py:156
  691.9 29.7 %shard_map.130 = (bf16[8,4,120,1536]{3,2,1,0:T(8,128)(2,1)}, bf16[8,4,120,1536]{3,2,1,0:T(8,128)(2,1)}) custom-call(f32[4,2,8,1,1024]{4,3,2,1,0:T(1,128)} %get-tuple-element.93.pos_ref, f32[4,2,8,1,1024]{4,3,2,1,0:T(1,128)} %get-tuple-element.92.wt_ref, bf16[4,1024,1536]{2,1,0:T(8,128)(2,1)} %bitcast.193), custom_call_target="tpu_custom_call" | custom-call | flops 24159191040 | bytes 37748736 | tf_op jit(solution)/shard_map/pallas_call | solution.py:42
  721.6 37.6 %all-to-all-done.8.rows1_ref = bf16[8,4,120,768]{3,2,1,0:T(8,128)(2,1)} async-done(((bf16[8,4,120,768]{3,2,1,0:T(8,128)(2,1)}), bf16[8,4,120,768]{3,2,1,0:T(8,128)(2,1)}, u32[]{:S(2)}, u32[]{:S(2)}) %all-to-all-start.8) | async-done | bytes 5898272 | tf_op jit(solution)/shard_map/all_to_all | solution.py:156
  764.5 29.3 %shard_map.129 = (f32[4,1024,768]{2,1,0:T(8,128)}, f32[4,2,8,1024]{3,2,1,0:T(8,128)}) custom-call(f32[4,2,8,1,1024]{4,3,2,1,0:T(1,128)} %get-tuple-element.93.pos_ref, f32[4,2,8,1,1024]{4,3,2,1,0:T(1,128)} %get-tuple-element.92.wt_ref, bf16[8,4,120,768]{3,2,1,0:T(8,128)(2,1)} %all-to-all-done.7.rows0_ref, bf16[8,4,120,768]{3,2,1,0:T(8,128)(2,1)} %all-to-all-done.8.rows1_ref, ...), custom_call_target="tpu_custom_call" | custom-call | flops 24159191040 | bytes 52428800 | tf_op jit(solution)/shard_map/pallas_call | solution.py:89
  793.8 101.1 %all-to-all-done.9 = bf16[8,4,120,1536]{3,2,1,0:T(8,128)(2,1)} async-done(((bf16[8,4,120,1536]{3,2,1,0:T(8,128)(2,1)}), bf16[8,4,120,1536]{3,2,1,0:T(8,128)(2,1)}, u32[]{:S(2)}, u32[]{:S(2)}) %all-to-all-start.9) | async-done | bytes 11796512 | tf_op jit(solution)/shard_map/all_to_all | solution.py:156
  900.7 15.5 fusion.3
  933.4 97.9 %all-to-all-done.10 = bf16[8,4,120,1536]{3,2,1,0:T(8,128)(2,1)} async-done(((bf16[8,4,120,1536]{3,2,1,0:T(8,128)(2,1)}), bf16[8,4,120,1536]{3,2,1,0:T(8,128)(2,1)}, u32[]{:S(2)}, u32[]{:S(2)}) %all-to-all-start.10) | async-done | bytes 11796512 | tf_op jit(solution)/shard_map/all_to_all | solution.py:156
  1035.7 15.7 fusion.7
  1060.3 11.0 all-to-all-done.11.rows0_ref
  1071.3 38.8 %all_to_all.107.rows1_ref = bf16[8,4,120,384]{3,2,1,0:T(8,128)(2,1)} all-to-all(bf16[8,4,120,384]{3,2,1,0:T(8,128)(2,1)S(1)} %bitcast.175), channel_id=1, replica_groups={{0,1,2,3,4,5,6,7},{8,9,10,11,12,13,14,15},{16,17,18,19,20,21,22,23},{24..., dimensions={0} | all-to-all | bytes 5898240 | tf_op jit(solution)/shard_map/all_to_all | solution.py:156
  1110.1 12.1 shard_map.131
  1144.1 18.3 %all-to-all-done.13.rows0_ref = bf16[8,4,120,384]{3,2,1,0:T(8,128)(2,1)} async-done(((bf16[8,4,120,384]{3,2,1,0:T(8,128)(2,1)}), bf16[8,4,120,384]{3,2,1,0:T(8,128)(2,1)}, u32[]{:S(2)}, u32[]{:S(2)}) %all-to-all-start.13) | async-done | bytes 2949152 | tf_op jit(solution)/shard_map/all_to_all | solution.py:156
  1162.3 38.8 %all_to_all.108.rows1_ref = bf16[8,4,120,384]{3,2,1,0:T(8,128)(2,1)} all-to-all(bf16[8,4,120,384]{3,2,1,0:T(8,128)(2,1)S(1)} %bitcast.176), channel_id=1, replica_groups={{0,1,2,3,4,5,6,7},{8,9,10,11,12,13,14,15},{16,17,18,19,20,21,22,23},{24..., dimensions={0} | all-to-all | bytes 5898240 | tf_op jit(solution)/shard_map/all_to_all | solution.py:156
  1201.1 12.1 shard_map.132
  1234.8 18.6 %all-to-all-done.15.rows0_ref = bf16[8,4,120,384]{3,2,1,0:T(8,128)(2,1)} async-done(((bf16[8,4,120,384]{3,2,1,0:T(8,128)(2,1)}), bf16[8,4,120,384]{3,2,1,0:T(8,128)(2,1)}, u32[]{:S(2)}, u32[]{:S(2)}) %all-to-all-start.15) | async-done | bytes 2949152 | tf_op jit(solution)/shard_map/all_to_all | solution.py:156
  1253.4 38.8 %all_to_all.109.rows1_ref = bf16[8,4,120,384]{3,2,1,0:T(8,128)(2,1)} all-to-all(bf16[8,4,120,384]{3,2,1,0:T(8,128)(2,1)S(1)} %bitcast.177), channel_id=1, replica_groups={{0,1,2,3,4,5,6,7},{8,9,10,11,12,13,14,15},{16,17,18,19,20,21,22,23},{24..., dimensions={0} | all-to-all | bytes 5898240 | tf_op jit(solution)/shard_map/all_to_all | solution.py:156
  1292.2 12.2 shard_map.133
  1318.7 25.8 %all-to-all-done.17.rows0_ref = bf16[8,4,120,384]{3,2,1,0:T(8,128)(2,1)} async-done(((bf16[8,4,120,384]{3,2,1,0:T(8,128)(2,1)}), bf16[8,4,120,384]{3,2,1,0:T(8,128)(2,1)}, u32[]{:S(2)}, u32[]{:S(2)}) %all-to-all-start.17) | async-done | bytes 2949152 | tf_op jit(solution)/shard_map/all_to_all | solution.py:156
  1351.5 33.1 %all-to-all-done.18.rows1_ref = bf16[8,4,120,384]{3,2,1,0:T(8,128)(2,1)} async-done(((bf16[8,4,120,384]{3,2,1,0:T(8,128)(2,1)}), bf16[8,4,120,384]{3,2,1,0:T(8,128)(2,1)}, u32[]{:S(2)}, u32[]{:S(2)}) %all-to-all-start.18) | async-done | bytes 2949152 | tf_op jit(solution)/shard_map/all_to_all | solution.py:156
  1384.6 12.2 shard_map.134
  1396.9 11.8 convolution_bitcast_fusion.1
  1416.3 7.8 convolution_bitcast_fusion.3
  1427.3 11.9 convolution_bitcast_fusion
  1439.2 11.0 convolution_bitcast_fusion.4
  1450.2 10.9 convolution_bitcast_fusion.2
  1465.2 8.8 pad_maximum_fusion.2
  1502.7 14.7 all-to-all-done.20
  1519.7 44.8 %all_gather.27 = f32[1536,64]{1,0:T(8,128)S(1)} all-gather(f32[48,64]{1,0:T(8,128)S(1)} %reduce_sum.79), channel_id=1, replica_groups=mesh['ep'=32] {'ep'}, dimensions={0}, use_global_device_ids=true | all-gather | bytes 405504 | tf_op jit(solution)/shard_map/all_gather | solution.py:235
  1565.5 16.9 %reduce-scatter.17.cloned.1.call-done = f32[1,1024,384]{2,1,0:T(8,128)} async-done(((f32[4,1024,384]{2,1,0:T(8,128)}), f32[1,1024,384]{2,1,0:T(8,128)}) %reduce-scatter.17.cloned.1.call-update) | async-done | bytes 1572880 | tf_op jit(solution)/shard_map/reduce_scatter | solution.py:164
  (182 shorter events, 217.1 us)
Async XLA Ops:
  7.2 128.9 %all-gather.7.cloned.1.call-start = ((), (), s32[]{:S(2)}) async-start(), calls=%async_computation.33 | async-start | bytes 7864320 | tf_op jit(solution)/shard_map/all_gather | solution.py:124
  11.2 240.0 %all-gather.9.cloned.1.call-start = ((), (), s32[]{:S(2)}) async-start(), calls=%async_computation.34 | async-start | bytes 7864320 | tf_op jit(solution)/shard_map/all_gather | solution.py:124
  12.6 139.5 %copy-start.24 = (pred[64,1024]{1,0:T(8,128)(4,1)}, pred[64,1024]{1,0:T(8,128)(4,1)S(1)}, u32[]{:S(2)}) copy-start(pred[64,1024]{1,0:T(8,128)(4,1)S(1)} %fusion.36) | copy-start | bytes 196612
  224.3 72.0 %all-to-all-start.2 = ((bf16[8,4,120,768]{3,2,1,0:T(8,128)(2,1)}), bf16[8,4,120,768]{3,2,1,0:T(8,128)(2,1)}, u32[]{:S(2)}, u32[]{:S(2)}) async-start(bf16[8,4,120,768]{3,2,1,0:T(8,128)(2,1)} %get-tuple-element.43), calls=%async_computation.2 | async-start | bytes 11796480 | tf_op jit(solution)/shard_map/all_to_all | solution.py:156
  296.3 72.0 %all-to-all-start.3 = ((bf16[8,4,120,768]{3,2,1,0:T(8,128)(2,1)}), bf16[8,4,120,768]{3,2,1,0:T(8,128)(2,1)}, u32[]{:S(2)}, u32[]{:S(2)}) async-start(bf16[8,4,120,768]{3,2,1,0:T(8,128)(2,1)} %get-tuple-element.44), calls=%async_computation.3 | async-start | bytes 11796480 | tf_op jit(solution)/shard_map/all_to_all | solution.py:156
  301.0 219.7 %all-gather.11.cloned.1.call-start = ((), (), s32[]{:S(2)}) async-start(), calls=%async_computation.35 | async-start | bytes 15728640 | tf_op jit(solution)/shard_map/all_gather | solution.py:125
  368.3 17.8 %slice-start = ((s8[5898240]{0:T(1024)(128)(4,1)}), s8[1703936]{0:T(1024)(128)(4,1)S(1)}, s32[]{:S(2)}) async-start(s8[5898240]{0:T(1024)(128)(4,1)} %bitcast.179), calls=%async_computation.36 | async-start | bytes 3407872
  368.3 72.6 %all-to-all-start.4 = ((bf16[8,4,120,768]{3,2,1,0:T(8,128)(2,1)}), bf16[8,4,120,768]{3,2,1,0:T(8,128)(2,1)}, u32[]{:S(2)}, u32[]{:S(2)}) async-start(bf16[8,4,120,768]{3,2,1,0:T(8,128)(2,1)} %get-tuple-element.46), calls=%async_computation.4 | async-start | bytes 11796480 | tf_op jit(solution)/shard_map/all_to_all | solution.py:156
  373.6 12.4 slice-start.1
  399.7 8.3 copy-start.37
  440.9 72.5 %all-to-all-start.5 = ((bf16[8,4,120,768]{3,2,1,0:T(8,128)(2,1)}), bf16[8,4,120,768]{3,2,1,0:T(8,128)(2,1)}, u32[]{:S(2)}, u32[]{:S(2)}) async-start(bf16[8,4,120,768]{3,2,1,0:T(8,128)(2,1)} %bitcast.187), calls=%async_computation.5 | async-start | bytes 11796480 | tf_op jit(solution)/shard_map/all_to_all | solution.py:156
  446.1 11.4 copy-start.22
  513.4 72.0 %all-to-all-start.6 = ((bf16[8,4,120,768]{3,2,1,0:T(8,128)(2,1)}), bf16[8,4,120,768]{3,2,1,0:T(8,128)(2,1)}, u32[]{:S(2)}, u32[]{:S(2)}) async-start(bf16[8,4,120,768]{3,2,1,0:T(8,128)(2,1)} %bitcast.188), calls=%async_computation.6 | async-start | bytes 11796480 | tf_op jit(solution)/shard_map/all_to_all | solution.py:156
  518.1 906.0 %reduce-scatter.7.cloned.1.call-start = ((), (), s32[]{:S(2)}) async-start(), calls=%async_computation.27 | async-start | bytes 15728640 | tf_op jit(solution)/shard_map/reduce_scatter | solution.py:164
  614.7 72.0 %all-to-all-start.7 = ((bf16[8,4,120,768]{3,2,1,0:T(8,128)(2,1)}), bf16[8,4,120,768]{3,2,1,0:T(8,128)(2,1)}, u32[]{:S(2)}, u32[]{:S(2)}) async-start(bf16[8,4,120,768]{3,2,1,0:T(8,128)(2,1)} %bitcast.186), calls=%async_computation.8 | async-start | bytes 11796480 | tf_op jit(solution)/shard_map/all_to_all | solution.py:156
  686.7 72.4 %all-to-all-start.8 = ((bf16[8,4,120,768]{3,2,1,0:T(8,128)(2,1)}), bf16[8,4,120,768]{3,2,1,0:T(8,128)(2,1)}, u32[]{:S(2)}, u32[]{:S(2)}) async-start(bf16[8,4,120,768]{3,2,1,0:T(8,128)(2,1)} %bitcast.189), calls=%async_computation.9 | async-start | bytes 11796480 | tf_op jit(solution)/shard_map/all_to_all | solution.py:156
  759.2 135.8 %all-to-all-start.9 = ((bf16[8,4,120,1536]{3,2,1,0:T(8,128)(2,1)}), bf16[8,4,120,1536]{3,2,1,0:T(8,128)(2,1)}, u32[]{:S(2)}, u32[]{:S(2)}) async-start(bf16[8,4,120,1536]{3,2,1,0:T(8,128)(2,1)} %get-tuple-element.55), calls=%async_computation.11 | async-start | bytes 23592960 | tf_op jit(solution)/shard_map/all_to_all | solution.py:156
  764.4 734.2 %reduce-scatter.9.cloned.1.call-start = ((), (), s32[]{:S(2)}) async-start(), calls=%async_computation.28 | async-start | bytes 15728640 | tf_op jit(solution)/shard_map/reduce_scatter | solution.py:164
  895.0 136.3 %all-to-all-start.10 = ((bf16[8,4,120,1536]{3,2,1,0:T(8,128)(2,1)}), bf16[8,4,120,1536]{3,2,1,0:T(8,128)(2,1)}, u32[]{:S(2)}, u32[]{:S(2)}) async-start(bf16[8,4,120,1536]{3,2,1,0:T(8,128)(2,1)} %get-tuple-element.57), calls=%async_computation.12 | async-start | bytes 23592960 | tf_op jit(solution)/shard_map/all_to_all | solution.py:156
  916.2 12.0 copy-start.1
  1031.2 40.1 %all-to-all-start.11 = ((bf16[8,4,120,384]{3,2,1,0:T(8,128)(2,1)}), bf16[8,4,120,384]{3,2,1,0:T(8,128)(2,1)}, u32[]{:S(2)}, u32[]{:S(2)}) async-start(bf16[8,4,120,384]{3,2,1,0:T(8,128)(2,1)} %bitcast.29), calls=%async_computation.13 | async-start | bytes 5898240 | tf_op jit(solution)/shard_map/all_to_all | solution.py:156
  1035.7 529.8 %reduce-scatter.11.cloned.1.call-start = ((), (), s32[]{:S(2)}) async-start(), calls=%async_computation.29 | async-start | bytes 7864320 | tf_op jit(solution)/shard_map/reduce_scatter | solution.py:164
  1122.3 40.1 %all-to-all-start.13 = ((bf16[8,4,120,384]{3,2,1,0:T(8,128)(2,1)}), bf16[8,4,120,384]{3,2,1,0:T(8,128)(2,1)}, u32[]{:S(2)}, u32[]{:S(2)}) async-start(bf16[8,4,120,384]{3,2,1,0:T(8,128)(2,1)} %bitcast.38), calls=%async_computation.16 | async-start | bytes 5898240 | tf_op jit(solution)/shard_map/all_to_all | solution.py:156
  1126.7 438.8 %reduce-scatter.13.cloned.1.call-start = ((), (), s32[]{:S(2)}) async-start(), calls=%async_computation.30 | async-start | bytes 7864320 | tf_op jit(solution)/shard_map/reduce_scatter | solution.py:164
  1213.3 40.1 %all-to-all-start.15 = ((bf16[8,4,120,384]{3,2,1,0:T(8,128)(2,1)}), bf16[8,4,120,384]{3,2,1,0:T(8,128)(2,1)}, u32[]{:S(2)}, u32[]{:S(2)}) async-start(bf16[8,4,120,384]{3,2,1,0:T(8,128)(2,1)} %bitcast.45), calls=%async_computation.19 | async-start | bytes 5898240 | tf_op jit(solution)/shard_map/all_to_all | solution.py:156
  1217.7 347.7 %reduce-scatter.15.cloned.1.call-start = ((), (), s32[]{:S(2)}) async-start(), calls=%async_computation.31 | async-start | bytes 7864320 | tf_op jit(solution)/shard_map/reduce_scatter | solution.py:164
  1304.4 40.1 %all-to-all-start.17 = ((bf16[8,4,120,384]{3,2,1,0:T(8,128)(2,1)}), bf16[8,4,120,384]{3,2,1,0:T(8,128)(2,1)}, u32[]{:S(2)}, u32[]{:S(2)}) async-start(bf16[8,4,120,384]{3,2,1,0:T(8,128)(2,1)} %bitcast.52), calls=%async_computation.22 | async-start | bytes 5898240 | tf_op jit(solution)/shard_map/all_to_all | solution.py:156
  1318.7 30.7 %copy-start.35 = (f32[128]{0:T(128)S(1)}, f32[128]{0:T(128)}, u32[]{:S(2)}) copy-start(f32[128]{0:T(128)} %psum.7) | copy-start | bytes 1540
  1318.7 32.0 %copy-start.26 = (f32[4,2,8,1024]{3,2,1,0:T(8,128)S(1)}, f32[4,2,8,1024]{3,2,1,0:T(8,128)}, u32[]{:S(2)}) copy-start(f32[4,2,8,1024]{3,2,1,0:T(8,128)} %get-tuple-element.66) | copy-start | bytes 786436
  1318.7 32.1 %copy-start.27 = (f32[4,2,8,1024]{3,2,1,0:T(8,128)S(1)}, f32[4,2,8,1024]{3,2,1,0:T(8,128)}, u32[]{:S(2)}) copy-start(f32[4,2,8,1024]{3,2,1,0:T(8,128)} %get-tuple-element.67) | copy-start | bytes 786436
  1344.5 40.1 %all-to-all-start.18 = ((bf16[8,4,120,384]{3,2,1,0:T(8,128)(2,1)}), bf16[8,4,120,384]{3,2,1,0:T(8,128)(2,1)}, u32[]{:S(2)}, u32[]{:S(2)}) async-start(bf16[8,4,120,384]{3,2,1,0:T(8,128)(2,1)} %bitcast.55), calls=%async_computation.23 | async-start | bytes 5898240 | tf_op jit(solution)/shard_map/all_to_all | solution.py:156
  1349.0 233.4 %reduce-scatter.17.cloned.1.call-start = ((), (), s32[]{:S(2)}) async-start(), calls=%async_computation.32 | async-start | bytes 7864320 | tf_op jit(solution)/shard_map/reduce_scatter | solution.py:164
  1396.8 11.8 slice-start.2
  1396.8 11.8 copy-start.11
  1396.8 11.8 slice-start.3
  1408.6 7.7 copy-start.4
  1427.3 11.9 copy-start.15
  1439.2 11.0 copy-start.9
  1461.1 17.8 %all-to-all-start.19 = ((f32[4,2,8,1024]{3,2,1,0:T(8,128)}), f32[4,2,8,1024]{3,2,1,0:T(8,128)}, u32[]{:S(2)}, u32[]{:S(2)}) async-start(f32[4,2,8,1024]{3,2,1,0:T(8,128)} %add.81), calls=%async_computation.25 | async-start | bytes 524288 | tf_op jit(solution)/shard_map/all_to_all | solution.py:223
  1465.1 17.5 %copy-start.25 = (pred[64,1024]{1,0:T(8,128)(4,1)S(1)}, pred[64,1024]{1,0:T(8,128)(4,1)}, u32[]{:S(2)}) copy-start(pred[64,1024]{1,0:T(8,128)(4,1)} %copy-done.24) | copy-start | bytes 196612
  1465.1 17.5 %copy-start.29 = (f32[1024]{0:T(1024)S(1)}, f32[1024]{0:T(1024)}, u32[]{:S(2)}) copy-start(f32[1024]{0:T(1024)} %copy-done.28) | copy-start | bytes 12292
  1465.1 17.5 %copy-start.31 = (f32[1024]{0:T(1024)S(1)}, f32[1024]{0:T(1024)}, u32[]{:S(2)}) copy-start(f32[1024]{0:T(1024)} %copy-done.30) | copy-start | bytes 12292
  1465.1 17.4 %copy-start.33 = (f32[1024]{0:T(1024)S(1)}, f32[1024]{0:T(1024)}, u32[]{:S(2)}) copy-start(f32[1024]{0:T(1024)} %copy-done.32) | copy-start | bytes 12292
  1465.2 19.8 %copy-start.17 = (bf16[1024,1536]{1,0:T(8,128)(2,1)S(1)}, bf16[1024,1536]{1,0:T(8,128)(2,1)}, u32[]{:S(2)}) copy-start(bf16[1024,1536]{1,0:T(8,128)(2,1)} %param.7) | copy-start | bytes 9437188
  1489.9 27.4 %all-to-all-start.20 = ((f32[32,1,3072]{2,1,0:T(1,128)}), f32[32,1,3072]{2,1,0:T(1,128)S(1)}, u32[]{:S(2)}, u32[]{:S(2)}) async-start(f32[32,1,3072]{2,1,0:T(1,128)} %reshape.110), calls=%async_computation.26 | async-start | bytes 786432 | tf_op jit(solution)/shard_map/all_to_all | solution.py:234
  1492.6 8.2 copy-start.20
  1500.7 81.6 %copy-start.19 = (f32[64,1024]{1,0:T(8,128)S(1)}, f32[64,1024]{1,0:T(8,128)}, u32[]{:S(2)}) copy-start(f32[64,1024]{1,0:T(8,128)} %copy-done.18) | copy-start | bytes 786436
  1500.7 81.6 %copy-start.23 = (f32[64,1024]{1,0:T(8,128)S(1)}, f32[64,1024]{1,0:T(8,128)}, u32[]{:S(2)}) copy-start(f32[64,1024]{1,0:T(8,128)} %reshape.104) | copy-start | bytes 786436
  (20 other events, 74.4 us)
Sparse Core Ops, SparseCore 0:
  11.3 124.7 all-gather.6
  138.2 112.9 all-gather.8
  303.4 217.2 all-gather.10
  614.8 207.9 reduce-scatter.6
  825.0 212.4 reduce-scatter.8
  1122.4 106.8 reduce-scatter.10
  1231.6 111.2 reduce-scatter.12
  1345.2 111.2 reduce-scatter.14
  1458.8 123.5 reduce-scatter.16
